TPU v7x, 32 devices: a whole 2x2x4 slice. The times are simulated.
32 devices in a mesh: layer: 8 (over y, x, core), latent: 4 (over z).
Axes of the slice: x: 2, y: 2, z: 4, core: 2. Of those that a mesh axis runs over, the one named last changes fastest.
Arguments:
- decoder: bfloat16 [65536, 4, 2304], P(('layer', 'latent')), may hold values from -0.375 to 0.375
- code_index: int32 [4, 128, 64], replicated, may hold values from 0 to 16383, all different within a row
- code_value: bfloat16 [4, 128, 64], replicated, may hold values from 0.19921875 to 4
- bias: float32 [4, 2304], replicated, may hold values from -3 to 3
- target: bfloat16 [4, 128, 2304], replicated, may hold values from -6 to 6
Outputs:
- layer_error: float32 [4], replicated
- grad_decoder: bfloat16 [65536, 4, 2304], P(('layer', 'latent'))
- code_grad: float32 [4, 128, 64], replicated
Inputs may be any that keep to these rules, and one draw needn't show every extreme that they name: `code_index`: the 64 indices of one token in one layer are distinct.
All inputs are finite; a program needn't handle non-finite values.
Results may differ from a plain program's by a relative error of at most 0.0048.
Values may be sent and summed in bfloat16 or wider, within the bound.
No kernel may reach another device: no remote copies, remote signals or barrier semaphores. Data moves between devices by JAX's collectives and lax.ppermute only.
A program may use at most 192 MiB of HBM per device.

v0:
```python
import jax
import jax.numpy as jnp
from jax import lax
from jax.sharding import PartitionSpec as P

D = 2304
LAYERS = 4
TOPK = 64
TOKENS = 128


def build_codes(index_rows, value_rows, offset, slab_width):
    columns = offset + lax.iota(jnp.int32, slab_width)
    matches = index_rows[:, :, None] == columns[None, None, :]
    dense = jnp.sum(jnp.where(matches, value_rows[:, :, None].astype(jnp.float32), 0.0), axis=1)
    return (matches, dense.astype(jnp.bfloat16))


def contract_rows(left, right):
    return lax.dot_general(
        left, right, (((0,), (0,)), ((), ())), preferred_element_type=jnp.float32
    )


def contract_cols(left, right):
    return lax.dot_general(
        left, right, (((1,), (1,)), ((), ())), preferred_element_type=jnp.float32
    )


def on_device(decoder, code_index, code_value, bias, target):
    layer_count = lax.axis_size("layer")
    latent_count = lax.axis_size("latent")
    group_size = layer_count // LAYERS
    slab_width = decoder.shape[0]
    layer_pos = lax.axis_index("layer")
    source = layer_pos // group_size
    offset = (layer_pos % group_size * latent_count + lax.axis_index("latent")) * slab_width
    matches, dense_codes = build_codes(
        lax.dynamic_index_in_dim(code_index, source, 0, keepdims=False),
        lax.dynamic_index_in_dim(code_value, source, 0, keepdims=False),
        offset,
        slab_width,
    )

    def forward_step(target_layer, totals):
        weight_slab = lax.dynamic_index_in_dim(decoder, target_layer, 1, keepdims=False)
        product = jnp.dot(dense_codes, weight_slab, preferred_element_type=jnp.float32)
        return lax.dynamic_update_index_in_dim(totals, product, target_layer, 0)

    partials = jnp.zeros((LAYERS, TOKENS, D), jnp.float32)
    stop_at = LAYERS
    partials = lax.fori_loop(source, stop_at, forward_step, partials)
    recon_sum = lax.psum(partials, ("layer", "latent"))
    residual = recon_sum + bias[:, None, :] - target.astype(jnp.float32)
    layer_error = jnp.mean(residual * residual, axis=(1, 2))
    error_b = residual.astype(jnp.bfloat16)

    def backward_step(target_layer, state_pair):
        grads, code_sums = state_pair
        weight_slab = lax.dynamic_index_in_dim(decoder, target_layer, 1, keepdims=False)
        target_error = lax.dynamic_index_in_dim(error_b, target_layer, 0, keepdims=False)
        grad_block = contract_rows(dense_codes, target_error).astype(jnp.bfloat16)
        grads = lax.dynamic_update_index_in_dim(grads, grad_block, target_layer, 1)
        return (grads, code_sums + contract_cols(target_error, weight_slab))

    start_pair = (
        jnp.zeros(decoder.shape, jnp.bfloat16),
        jnp.zeros((TOKENS, slab_width), jnp.float32),
    )
    grads, code_sums = lax.fori_loop(source, stop_at, backward_step, start_pair)
    picked = jnp.sum(jnp.where(matches, code_sums[:, None, :], 0.0), axis=2)
    code_parts = lax.dynamic_update_index_in_dim(
        jnp.zeros((LAYERS, TOKENS, TOPK), jnp.float32), picked, source, 0
    )
    code_grad = lax.psum(code_parts, ("layer", "latent"))
    return (layer_error, grads, code_grad)


def solution(mesh):
    placed = (P(("layer", "latent"), None, None), P(), P(), P(), P())
    return jax.shard_map(
        on_device,
        mesh=mesh,
        in_specs=placed,
        out_specs=(P(), P(("layer", "latent"), None, None), P()),
        check_vma=False,
    )
```

profile of v0, /device:TPU:0, one launch (start us, length us, event | category | flops | bytes accessed | tf_op | source)
XLA Modules:
  0.0 428.5 jit_solution(2103701920801345203)
XLA Ops:
  7.2 0.0 copy-start
  7.2 0.0 all-reduce.3.cloned.1.call-start
  7.2 25.9 %copy.19 = bf16[2048,4,2304]{2,0,1:T(8,128)(2,1)} copy(bf16[2048,4,2304]{2,1,0:T(4,128)(2,1)} %param.9) | data formatting | bytes 75497472 | tf_op jit(solution)/shard_map/while | solution.py:53
  33.1 0.7 bitcast_convert_fusion
  33.8 0.1 copy.18
  34.0 0.0 copy-done
  34.0 0.1 copy.17
  34.1 9.8 %fusion.21 = bf16[128,2048]{1,0:T(8,128)(2,1)S(1)} fusion(f32[128,64]{1,0:T(8,128)S(1)} %copy.18, s32[2048]{0:T(1024)S(1)} %iota_add_fusion, s32[128,64]{1,0:T(8,128)S(1)} %copy.17), kind=kLoop, calls=%fused_computation.21 | loop fusion | flops 50069504 | bytes 598016 | tf_op jit(solution)/shard_map/reduce_sum | solution.py:15
  43.9 2.6 broadcast_in_dim.51.clone
  46.5 26.9 %while.22 = (s32[]{:T(128)}, f32[4,128,2304]{2,1,0:T(8,128)}, bf16[2048,4,2304]{2,0,1:T(8,128)(2,1)}, bf16[128,2048]{1,0:T(8,128)(2,1)S(1)}, s32[]{:T(128)}, /*index=5*/s32[]{:T(128)}, s32[]{:T(128)}) while((s32[]{:T(128)}, f32[4,128,2304]{2,1,0:T(8,128)}, bf16[2048,4,2304]{2,0,1:T(8,128)(2,1)}, bf16[128,2048]{1,0:T(8,128)(2,1)S(1)}, ...), condition=%wide.region_2.3_spmd, body=%wide.region_1.2_spmd.sunk | while | flops 1207959552 | bytes 15859839 | solution.py:53
  46.5 5.2 %fusion.37 = f32[1,128,2304]{1,2,0:T(8,128)S(1)} fusion(bf16[128,2048]{1,0:T(8,128)(2,1)S(1)} %get-tuple-element.191, bf16[2048,4,2304]{2,0,1:T(8,128)(2,1)} %get-tuple-element.190, s32[]{:T(128)S(6)} %select_n.53), kind=kOutput, calls=%fused_computation.3.clone.1 | convolution fusion | flops 1207959552 | bytes 11141124 | tf_op jit(solution)/shard_map/while/body/dot_general | solution.py:48
  51.7 0.4 copy.30
  52.1 1.1 constant_dynamic-update-slice_fusion.3
  53.2 5.2 %fusion.37 = f32[1,128,2304]{1,2,0:T(8,128)S(1)} fusion(bf16[128,2048]{1,0:T(8,128)(2,1)S(1)} %get-tuple-element.191, bf16[2048,4,2304]{2,0,1:T(8,128)(2,1)} %get-tuple-element.190, s32[]{:T(128)S(6)} %select_n.53), kind=kOutput, calls=%fused_computation.3.clone.1 | convolution fusion | flops 1207959552 | bytes 11141124 | tf_op jit(solution)/shard_map/while/body/dot_general | solution.py:48
  58.4 0.4 copy.30
  58.8 1.1 constant_dynamic-update-slice_fusion.3
  59.9 5.2 %fusion.37 = f32[1,128,2304]{1,2,0:T(8,128)S(1)} fusion(bf16[128,2048]{1,0:T(8,128)(2,1)S(1)} %get-tuple-element.191, bf16[2048,4,2304]{2,0,1:T(8,128)(2,1)} %get-tuple-element.190, s32[]{:T(128)S(6)} %select_n.53), kind=kOutput, calls=%fused_computation.3.clone.1 | convolution fusion | flops 1207959552 | bytes 11141124 | tf_op jit(solution)/shard_map/while/body/dot_general | solution.py:48
  65.1 0.4 copy.30
  65.5 1.1 constant_dynamic-update-slice_fusion.3
  66.6 5.2 %fusion.37 = f32[1,128,2304]{1,2,0:T(8,128)S(1)} fusion(bf16[128,2048]{1,0:T(8,128)(2,1)S(1)} %get-tuple-element.191, bf16[2048,4,2304]{2,0,1:T(8,128)(2,1)} %get-tuple-element.190, s32[]{:T(128)S(6)} %select_n.53), kind=kOutput, calls=%fused_computation.3.clone.1 | convolution fusion | flops 1207959552 | bytes 11141124 | tf_op jit(solution)/shard_map/while/body/dot_general | solution.py:48
  71.8 0.4 copy.30
  72.2 1.2 constant_dynamic-update-slice_fusion.3
  73.4 0.0 all-reduce.3.cloned.1.call-update
  73.4 0.0 all-reduce.5.cloned.1.call-start
  73.5 145.7 %all-reduce.3.cloned.1.call-done = f32[4,128,2304]{2,1,0:T(8,128)} async-done(((f32[4,128,2304]{2,1,0:T(8,128)}), f32[4,128,2304]{2,1,0:T(8,128)}) %all-reduce.3.cloned.1.call-update) | async-done | bytes 4718608 | tf_op jit(solution)/shard_map/psum | solution.py:54
  219.2 0.0 copy-done.4
  219.2 4.1 fusion.23
  223.3 0.0 copy-done.2
  223.3 12.5 %broadcast_in_dim.54 = bf16[2048,4,2304]{0,2,1:T(8,128)(2,1)} broadcast(bf16[]{:T(256)} %constant.88.clone.1), dimensions={} | broadcast | bytes 37748736 | tf_op jit(solution)/shard_map/broadcast_in_dim | solution.py:68
  235.8 0.1 broadcast_in_dim.55
  235.9 52.3 %while.23 = (s32[]{:T(128)}, bf16[2048,4,2304]{0,2,1:T(8,128)(2,1)}, f32[128,2048]{1,0:T(8,128)S(1)}, bf16[4,128,2304]{2,1,0:T(8,128)(2,1)S(1)}, bf16[128,2048]{...) while((s32[]{:T(128)}, bf16[2048,4,2304]{0,2,1:T(8,128)(2,1)}, ...), condition=%wide.region_6.7_spmd, body=%wide.region_5.6_spmd.sunk | while | flops 2420899840 | bytes 22677640 | solution.py:71
  236.0 6.1 %fusion.42 = bf16[2048,4,2304]{0,2,1:T(8,128)(2,1)} fusion(bf16[2048,4,2304]{0,2,1:T(8,128)(2,1)} %get-tuple-element.205, s32[]{:T(128)S(6)} %select_n.54, bf16[128,2048]{1,0:T(8,128)(2,1)} %get-tuple-element.217, bf16[4,128,2304]{2,1,0:T(8,128)(2,1)S(1)} %get-tuple-element.216), kind=kOutput, calls=%fused_computation.8.clone.1 | convolution fusion | flops 1212678144 | bytes 10552320 | tf_op jit(solution)/shard_map/while/body/dot_general | solution.py:20
  242.1 6.9 %fusion.43 = f32[128,2048]{1,0:T(8,128)S(1)} fusion(f32[128,2048]{1,0:T(8,128)S(1)} %get-tuple-element.206, bf16[2048,4,2304]{2,0,1:T(8,128)(2,1)} %get-tuple-element.218, s32[]{:T(128)S(6)} %select_n.54, bf16[4,128,2304]{2,1,0:T(8,128)(2,1)S(1)} %get-tuple-element.216), kind=kOutput, calls=%fused_computation.12.clone.1 | convolution fusion | flops 1208221696 | bytes 12125184 | tf_op jit(solution)/shard_map/while/body/dot_general | solution.py:26
  249.0 6.1 %fusion.42 = bf16[2048,4,2304]{0,2,1:T(8,128)(2,1)} fusion(bf16[2048,4,2304]{0,2,1:T(8,128)(2,1)} %get-tuple-element.205, s32[]{:T(128)S(6)} %select_n.54, bf16[128,2048]{1,0:T(8,128)(2,1)} %get-tuple-element.217, bf16[4,128,2304]{2,1,0:T(8,128)(2,1)S(1)} %get-tuple-element.216), kind=kOutput, calls=%fused_computation.8.clone.1 | convolution fusion | flops 1212678144 | bytes 10552320 | tf_op jit(solution)/shard_map/while/body/dot_general | solution.py:20
  255.1 6.9 %fusion.43 = f32[128,2048]{1,0:T(8,128)S(1)} fusion(f32[128,2048]{1,0:T(8,128)S(1)} %get-tuple-element.206, bf16[2048,4,2304]{2,0,1:T(8,128)(2,1)} %get-tuple-element.218, s32[]{:T(128)S(6)} %select_n.54, bf16[4,128,2304]{2,1,0:T(8,128)(2,1)S(1)} %get-tuple-element.216), kind=kOutput, calls=%fused_computation.12.clone.1 | convolution fusion | flops 1208221696 | bytes 12125184 | tf_op jit(solution)/shard_map/while/body/dot_general | solution.py:26
  262.1 6.2 %fusion.42 = bf16[2048,4,2304]{0,2,1:T(8,128)(2,1)} fusion(bf16[2048,4,2304]{0,2,1:T(8,128)(2,1)} %get-tuple-element.205, s32[]{:T(128)S(6)} %select_n.54, bf16[128,2048]{1,0:T(8,128)(2,1)} %get-tuple-element.217, bf16[4,128,2304]{2,1,0:T(8,128)(2,1)S(1)} %get-tuple-element.216), kind=kOutput, calls=%fused_computation.8.clone.1 | convolution fusion | flops 1212678144 | bytes 10552320 | tf_op jit(solution)/shard_map/while/body/dot_general | solution.py:20
  268.3 6.9 %fusion.43 = f32[128,2048]{1,0:T(8,128)S(1)} fusion(f32[128,2048]{1,0:T(8,128)S(1)} %get-tuple-element.206, bf16[2048,4,2304]{2,0,1:T(8,128)(2,1)} %get-tuple-element.218, s32[]{:T(128)S(6)} %select_n.54, bf16[4,128,2304]{2,1,0:T(8,128)(2,1)S(1)} %get-tuple-element.216), kind=kOutput, calls=%fused_computation.12.clone.1 | convolution fusion | flops 1208221696 | bytes 12125184 | tf_op jit(solution)/shard_map/while/body/dot_general | solution.py:26
  275.2 6.1 %fusion.42 = bf16[2048,4,2304]{0,2,1:T(8,128)(2,1)} fusion(bf16[2048,4,2304]{0,2,1:T(8,128)(2,1)} %get-tuple-element.205, s32[]{:T(128)S(6)} %select_n.54, bf16[128,2048]{1,0:T(8,128)(2,1)} %get-tuple-element.217, bf16[4,128,2304]{2,1,0:T(8,128)(2,1)S(1)} %get-tuple-element.216), kind=kOutput, calls=%fused_computation.8.clone.1 | convolution fusion | flops 1212678144 | bytes 10552320 | tf_op jit(solution)/shard_map/while/body/dot_general | solution.py:20
  281.3 6.9 %fusion.43 = f32[128,2048]{1,0:T(8,128)S(1)} fusion(f32[128,2048]{1,0:T(8,128)S(1)} %get-tuple-element.206, bf16[2048,4,2304]{2,0,1:T(8,128)(2,1)} %get-tuple-element.218, s32[]{:T(128)S(6)} %select_n.54, bf16[4,128,2304]{2,1,0:T(8,128)(2,1)S(1)} %get-tuple-element.216), kind=kOutput, calls=%fused_computation.12.clone.1 | convolution fusion | flops 1208221696 | bytes 12125184 | tf_op jit(solution)/shard_map/while/body/dot_general | solution.py:26
  288.2 9.0 %fusion.22 = f32[128,64]{1,0:T(8,128)S(1)} fusion(f32[128,2048]{1,0:T(8,128)S(1)} %get-tuple-element.60, s32[2048]{0:T(1024)S(1)} %iota_add_fusion, s32[128,64]{1,0:T(8,128)S(1)} %copy.17), kind=kLoop, calls=%fused_computation.22 | loop fusion | flops 50323456 | bytes 1122304 | tf_op jit(solution)/shard_map/reduce_sum | solution.py:72
  297.2 0.1 copy.22
  297.4 0.0 copy-start.3
  297.4 0.6 copy-done.3
  298.0 0.0 all-reduce.5.cloned.1.call-update
  298.0 0.5 broadcast_multiply_fusion
  298.6 57.6 %copy.23 = bf16[2048,4,2304]{2,1,0:T(4,128)(2,1)} copy(bf16[2048,4,2304]{0,2,1:T(8,128)(2,1)} %get-tuple-element.88) | data formatting | bytes 75497472
  356.2 63.9 %all-reduce.5.cloned.1.call-done = f32[4,128,64]{1,2,0:T(8,128)} async-done(((f32[4,128,64]{1,2,0:T(8,128)}), f32[4,128,64]{1,2,0:T(8,128)}) %all-reduce.5.cloned.1.call-update) | async-done | bytes 131088 | tf_op jit(solution)/shard_map/psum | solution.py:76
  420.1 1.6 copy.51
  (8 shorter events, 0.1 us)
Async XLA Ops:
  7.2 26.8 %copy-start = (s32[4,128,64]{1,2,0:T(8,128)S(1)}, s32[4,128,64]{1,2,0:T(8,128)}, u32[]{:S(2)}) copy-start(s32[4,128,64]{1,2,0:T(8,128)} %param.10) | copy-start | bytes 393220
  7.2 212.0 %all-reduce.3.cloned.1.call-start = ((), (), s32[]{:S(2)}) async-start(), calls=%async_computation | async-start | bytes 9437184 | tf_op jit(solution)/shard_map/psum | solution.py:54
  46.5 172.7 %copy-start.4 = (f32[4,2304]{1,0:T(4,128)S(1)}, f32[4,2304]{1,0:T(4,128)}, u32[]{:S(2)}) copy-start(f32[4,2304]{1,0:T(4,128)} %param.12) | copy-start | bytes 110596
  73.4 149.9 %copy-start.2 = (bf16[128,2048]{1,0:T(8,128)(2,1)}, bf16[128,2048]{1,0:T(8,128)(2,1)S(1)}, u32[]{:S(2)}) copy-start(bf16[128,2048]{1,0:T(8,128)(2,1)S(1)} %get-tuple-element.230) | copy-start | bytes 1572868
  73.4 346.6 %all-reduce.5.cloned.1.call-start = ((), (), s32[]{:S(2)}) async-start(), calls=%async_computation.1 | async-start | bytes 262144 | tf_op jit(solution)/shard_map/psum | solution.py:76
  297.4 0.7 copy-start.3
  298.6 123.1 %copy-start.1 = (s32[4,128,64]{1,2,0:T(8,128)S(1)}, s32[4,128,64]{1,2,0:T(8,128)}, u32[]{:S(2)}) copy-start(s32[4,128,64]{1,2,0:T(8,128)} %param.10) | copy-start | bytes 393220
Sparse Core Ops, SparseCore 0:
  73.5 145.6 all-reduce.2
  298.2 121.8 all-reduce.4
where the time goes:
time: 430 us; the launch traced here: 428 us
  waiting for transfers between devices  210 us (49%)
  local copies, waits for them, and re-layouts  107 us (25%)
  matrix products  73 us (17%)
  other arithmetic  24.2 us (6%)
  between operations  14.2 us (3%)
    psum x1, waiting for transfers between devices, on_device(): recon_sum = lax.psum(partials, ('layer', 'latent'))  146 us
    psum x1, waiting for transfers between devices, on_device(): code_grad = lax.psum(code_parts, ('layer', 'latent'))  63.9 us
    unnamed x12, local copies, waits for them, and re-layouts  59.9 us
    dot_general x4, matrix products, contract_cols(): lax.dot_general(left, right, (((1,), (1,)), ((), ())), preferred_element_...  27.6 us
    while x1, local copies, waits for them, and re-layouts, on_device(): partials = lax.fori_loop(source, stop_at, forward_step, partials)  25.9 us
    dot_general x4, matrix products, contract_rows(): lax.dot_general(left, right, (((0,), (0,)), ((), ())), preferred_element_...  24.6 us
    dot_general x4, matrix products, forward_step(): jnp.dot(dense_codes, weight_slab, preferred_element_type=jnp.float32)  20.9 us
    broadcast_in_dim x1, local copies, waits for them, and re-layouts, on_device(): jnp.zeros(decoder.shape, jnp.bfloat16)  12.5 us
  transfers between devices with their start and end apart: 2, of which 2 were waited for; matrix products, arithmetic and copies ran while one was open for 14% of the time, Pallas kernels for 0%

commit v1 on v0

--- a/solution.py
+++ b/solution.py
@@ -1,3 +1,4 @@
+import functools
 import jax
 import jax.numpy as jnp
 from jax import lax
@@ -7,6 +8,13 @@
 LAYERS = 4
 TOPK = 64
 TOKENS = 128
+
+
+def detail_plate_for(x_part, net_axis):
+    return lax.all_gather(x_part, net_axis).sum(axis=0)
+
+
+_bind_sources_all = functools.partial(detail_plate_for, net_axis=("layer", "latent"))
 
 
 def build_codes(index_rows, value_rows, offset, slab_width):
@@ -73,7 +81,7 @@
     code_parts = lax.dynamic_update_index_in_dim(
         jnp.zeros((LAYERS, TOKENS, TOPK), jnp.float32), picked, source, 0
     )
-    code_grad = lax.psum(code_parts, ("layer", "latent"))
+    code_grad = _bind_sources_all(code_parts)
     return (layer_error, grads, code_grad)
 
 

time: 430 us -> 369 us (0.86)
  waiting for transfers between devices: 210 us -> 147 us
    psum x1 -> x0, waiting for transfers between devices: 63.9 us -> none  [on_device(): code_grad = lax.psum(code_parts, ('layer', 'latent'))]
    unnamed x12 -> x11, local copies, waits for them, and re-layouts: 59.9 us -> 58.5 us
  transfers between devices with their start and end apart: 2 -> 2, of which waited for: 2 -> 2; matrix products, arithmetic and copies ran while one was open for 14% -> 16% of each run, Pallas kernels for 0% -> 0%
where the time goes in v1:
time: 369 us; the launch traced here: 367 us
  waiting for transfers between devices  147 us (40%)
  local copies, waits for them, and re-layouts  106 us (29%)
  matrix products  73 us (20%)
  other arithmetic  27.3 us (7%)
  between operations  14.2 us (4%)
    psum x1, waiting for transfers between devices, on_device(): recon_sum = lax.psum(partials, ('layer', 'latent'))  146 us
    unnamed x11, local copies, waits for them, and re-layouts  58.5 us
    dot_general x4, matrix products, contract_cols(): lax.dot_general(left, right, (((1,), (1,)), ((), ())), preferred_element_...  27.6 us
    while x1, local copies, waits for them, and re-layouts, on_device(): partials = lax.fori_loop(source, stop_at, forward_step, partials)  25.9 us
    dot_general x4, matrix products, contract_rows(): lax.dot_general(left, right, (((0,), (0,)), ((), ())), preferred_element_...  24.6 us
    dot_general x4, matrix products, forward_step(): jnp.dot(dense_codes, weight_slab, preferred_element_type=jnp.float32)  20.9 us
    broadcast_in_dim x1, local copies, waits for them, and re-layouts, on_device(): jnp.zeros(decoder.shape, jnp.bfloat16)  12.5 us
    reduce_sum x1, other arithmetic, build_codes(): jnp.sum(jnp.where(matches, value_rows[:, :, None].astype(jnp.float32), 0....  9.81 us
  transfers between devices with their start and end apart: 2, of which 2 were waited for; matrix products, arithmetic and copies ran while one was open for 16% of the time, Pallas kernels for 0%

profile of v1, /device:TPU:0, one launch (start us, length us, event | category | flops | bytes accessed | tf_op | source)
XLA Modules:
  0.0 367.1 jit_solution(16275585443682882522)
XLA Ops:
  7.2 0.0 copy-start
  7.2 0.0 all-reduce.2.cloned.1.call-start
  7.2 25.9 %copy.25 = bf16[2048,4,2304]{2,0,1:T(8,128)(2,1)} copy(bf16[2048,4,2304]{2,1,0:T(4,128)(2,1)} %param.9) | data formatting | bytes 75497472 | tf_op jit(solution)/shard_map/while | solution.py:61
  33.1 0.7 bitcast_convert_fusion
  33.8 0.1 copy.24
  34.0 0.0 copy-done
  34.0 0.1 copy.23
  34.1 9.8 %fusion.21 = bf16[128,2048]{1,0:T(8,128)(2,1)S(1)} fusion(f32[128,64]{1,0:T(8,128)S(1)} %copy.24, s32[2048]{0:T(1024)S(1)} %iota_add_fusion, s32[128,64]{1,0:T(8,128)S(1)} %copy.23), kind=kLoop, calls=%fused_computation.21 | loop fusion | flops 50069504 | bytes 598016 | tf_op jit(solution)/shard_map/reduce_sum | solution.py:23
  43.9 2.6 broadcast_in_dim.49.clone
  46.5 26.9 %while.22 = (s32[]{:T(128)}, f32[4,128,2304]{2,1,0:T(8,128)}, bf16[2048,4,2304]{2,0,1:T(8,128)(2,1)}, bf16[128,2048]{1,0:T(8,128)(2,1)S(1)}, s32[]{:T(128)}, /*index=5*/s32[]{:T(128)}, s32[]{:T(128)}) while((s32[]{:T(128)}, f32[4,128,2304]{2,1,0:T(8,128)}, bf16[2048,4,2304]{2,0,1:T(8,128)(2,1)}, bf16[128,2048]{1,0:T(8,128)(2,1)S(1)}, ...), condition=%wide.region_2.3_spmd, body=%wide.region_1.2_spmd.sunk | while | flops 1207959552 | bytes 15859839 | solution.py:61
  46.5 5.2 %fusion.37 = f32[1,128,2304]{1,2,0:T(8,128)S(1)} fusion(bf16[128,2048]{1,0:T(8,128)(2,1)S(1)} %get-tuple-element.204, bf16[2048,4,2304]{2,0,1:T(8,128)(2,1)} %get-tuple-element.203, s32[]{:T(128)S(6)} %select_n.53), kind=kOutput, calls=%fused_computation.3.clone.1 | convolution fusion | flops 1207959552 | bytes 11141124 | tf_op jit(solution)/shard_map/while/body/dot_general | solution.py:56
  51.7 0.4 copy.37
  52.1 1.1 constant_dynamic-update-slice_fusion.3
  53.2 5.2 %fusion.37 = f32[1,128,2304]{1,2,0:T(8,128)S(1)} fusion(bf16[128,2048]{1,0:T(8,128)(2,1)S(1)} %get-tuple-element.204, bf16[2048,4,2304]{2,0,1:T(8,128)(2,1)} %get-tuple-element.203, s32[]{:T(128)S(6)} %select_n.53), kind=kOutput, calls=%fused_computation.3.clone.1 | convolution fusion | flops 1207959552 | bytes 11141124 | tf_op jit(solution)/shard_map/while/body/dot_general | solution.py:56
  58.4 0.4 copy.37
  58.8 1.1 constant_dynamic-update-slice_fusion.3
  59.9 5.2 %fusion.37 = f32[1,128,2304]{1,2,0:T(8,128)S(1)} fusion(bf16[128,2048]{1,0:T(8,128)(2,1)S(1)} %get-tuple-element.204, bf16[2048,4,2304]{2,0,1:T(8,128)(2,1)} %get-tuple-element.203, s32[]{:T(128)S(6)} %select_n.53), kind=kOutput, calls=%fused_computation.3.clone.1 | convolution fusion | flops 1207959552 | bytes 11141124 | tf_op jit(solution)/shard_map/while/body/dot_general | solution.py:56
  65.1 0.4 copy.37
  65.5 1.1 constant_dynamic-update-slice_fusion.3
  66.6 5.2 %fusion.37 = f32[1,128,2304]{1,2,0:T(8,128)S(1)} fusion(bf16[128,2048]{1,0:T(8,128)(2,1)S(1)} %get-tuple-element.204, bf16[2048,4,2304]{2,0,1:T(8,128)(2,1)} %get-tuple-element.203, s32[]{:T(128)S(6)} %select_n.53), kind=kOutput, calls=%fused_computation.3.clone.1 | convolution fusion | flops 1207959552 | bytes 11141124 | tf_op jit(solution)/shard_map/while/body/dot_general | solution.py:56
  71.8 0.4 copy.37
  72.2 1.2 constant_dynamic-update-slice_fusion.3
  73.4 0.0 all-reduce.2.cloned.1.call-update
  73.4 0.0 all-gather.2.cloned.1.call-start
  73.5 145.7 %all-reduce.2.cloned.1.call-done = f32[4,128,2304]{2,1,0:T(8,128)} async-done(((f32[4,128,2304]{2,1,0:T(8,128)}), f32[4,128,2304]{2,1,0:T(8,128)}) %all-reduce.2.cloned.1.call-update) | async-done | bytes 4718608 | tf_op jit(solution)/shard_map/psum | solution.py:62
  219.2 0.0 copy-done.4
  219.2 4.1 %fusion.23 = (bf16[4,128,2304]{2,1,0:T(8,128)(2,1)S(1)}, f32[4]{0:T(128)S(1)}) fusion(bf16[4,128,2304]{2,1,0:T(8,128)(2,1)} %param.13, f32[4,128,2304]{2,1,0:T(8,128)} %all-reduce.2.cloned.1.call-done, f32[4,2304]{1,0:T(4,128)S(1)} %copy-done.4), kind=kLoop, calls=%fused_computation.25 | loop fusion | flops 7077884 | bytes 9474064 | tf_op jit(solution)/shard_map/convert_element_type | solution.py:65
  223.3 12.5 %broadcast_in_dim.52 = bf16[2048,4,2304]{0,2,1:T(8,128)(2,1)} broadcast(bf16[]{:T(256)} %constant.89.clone.1), dimensions={} | broadcast | bytes 37748736 | tf_op jit(solution)/shard_map/broadcast_in_dim | solution.py:76
  235.8 0.1 broadcast_in_dim.53
  235.9 52.3 %while.23 = (s32[]{:T(128)}, bf16[2048,4,2304]{0,2,1:T(8,128)(2,1)}, f32[128,2048]{1,0:T(8,128)S(1)}, bf16[4,128,2304]{2,1,0:T(8,128)(2,1)S(1)}, bf16[128,2048]{...) while((s32[]{:T(128)}, bf16[2048,4,2304]{0,2,1:T(8,128)(2,1)}, ...), condition=%wide.region_6.7_spmd, body=%wide.region_5.6_spmd.sunk | while | flops 2420899840 | bytes 22677640 | solution.py:79
  236.0 6.1 %fusion.42 = bf16[2048,4,2304]{0,2,1:T(8,128)(2,1)} fusion(bf16[2048,4,2304]{0,2,1:T(8,128)(2,1)} %get-tuple-element.218, s32[]{:T(128)S(6)} %select_n.54, bf16[128,2048]{1,0:T(8,128)(2,1)} %get-tuple-element.230, bf16[4,128,2304]{2,1,0:T(8,128)(2,1)S(1)} %get-tuple-element.229), kind=kOutput, calls=%fused_computation.8.clone.1 | convolution fusion | flops 1212678144 | bytes 10552320 | tf_op jit(solution)/shard_map/while/body/dot_general | solution.py:28
  242.1 6.9 %fusion.43 = f32[128,2048]{1,0:T(8,128)S(1)} fusion(f32[128,2048]{1,0:T(8,128)S(1)} %get-tuple-element.219, bf16[2048,4,2304]{2,0,1:T(8,128)(2,1)} %get-tuple-element.231, s32[]{:T(128)S(6)} %select_n.54, bf16[4,128,2304]{2,1,0:T(8,128)(2,1)S(1)} %get-tuple-element.229), kind=kOutput, calls=%fused_computation.12.clone.1 | convolution fusion | flops 1208221696 | bytes 12125184 | tf_op jit(solution)/shard_map/while/body/dot_general | solution.py:34
  249.0 6.1 %fusion.42 = bf16[2048,4,2304]{0,2,1:T(8,128)(2,1)} fusion(bf16[2048,4,2304]{0,2,1:T(8,128)(2,1)} %get-tuple-element.218, s32[]{:T(128)S(6)} %select_n.54, bf16[128,2048]{1,0:T(8,128)(2,1)} %get-tuple-element.230, bf16[4,128,2304]{2,1,0:T(8,128)(2,1)S(1)} %get-tuple-element.229), kind=kOutput, calls=%fused_computation.8.clone.1 | convolution fusion | flops 1212678144 | bytes 10552320 | tf_op jit(solution)/shard_map/while/body/dot_general | solution.py:28
  255.1 6.9 %fusion.43 = f32[128,2048]{1,0:T(8,128)S(1)} fusion(f32[128,2048]{1,0:T(8,128)S(1)} %get-tuple-element.219, bf16[2048,4,2304]{2,0,1:T(8,128)(2,1)} %get-tuple-element.231, s32[]{:T(128)S(6)} %select_n.54, bf16[4,128,2304]{2,1,0:T(8,128)(2,1)S(1)} %get-tuple-element.229), kind=kOutput, calls=%fused_computation.12.clone.1 | convolution fusion | flops 1208221696 | bytes 12125184 | tf_op jit(solution)/shard_map/while/body/dot_general | solution.py:34
  262.1 6.2 %fusion.42 = bf16[2048,4,2304]{0,2,1:T(8,128)(2,1)} fusion(bf16[2048,4,2304]{0,2,1:T(8,128)(2,1)} %get-tuple-element.218, s32[]{:T(128)S(6)} %select_n.54, bf16[128,2048]{1,0:T(8,128)(2,1)} %get-tuple-element.230, bf16[4,128,2304]{2,1,0:T(8,128)(2,1)S(1)} %get-tuple-element.229), kind=kOutput, calls=%fused_computation.8.clone.1 | convolution fusion | flops 1212678144 | bytes 10552320 | tf_op jit(solution)/shard_map/while/body/dot_general | solution.py:28
  268.3 6.9 %fusion.43 = f32[128,2048]{1,0:T(8,128)S(1)} fusion(f32[128,2048]{1,0:T(8,128)S(1)} %get-tuple-element.219, bf16[2048,4,2304]{2,0,1:T(8,128)(2,1)} %get-tuple-element.231, s32[]{:T(128)S(6)} %select_n.54, bf16[4,128,2304]{2,1,0:T(8,128)(2,1)S(1)} %get-tuple-element.229), kind=kOutput, calls=%fused_computation.12.clone.1 | convolution fusion | flops 1208221696 | bytes 12125184 | tf_op jit(solution)/shard_map/while/body/dot_general | solution.py:34
  275.2 6.1 %fusion.42 = bf16[2048,4,2304]{0,2,1:T(8,128)(2,1)} fusion(bf16[2048,4,2304]{0,2,1:T(8,128)(2,1)} %get-tuple-element.218, s32[]{:T(128)S(6)} %select_n.54, bf16[128,2048]{1,0:T(8,128)(2,1)} %get-tuple-element.230, bf16[4,128,2304]{2,1,0:T(8,128)(2,1)S(1)} %get-tuple-element.229), kind=kOutput, calls=%fused_computation.8.clone.1 | convolution fusion | flops 1212678144 | bytes 10552320 | tf_op jit(solution)/shard_map/while/body/dot_general | solution.py:28
  281.3 6.9 %fusion.43 = f32[128,2048]{1,0:T(8,128)S(1)} fusion(f32[128,2048]{1,0:T(8,128)S(1)} %get-tuple-element.219, bf16[2048,4,2304]{2,0,1:T(8,128)(2,1)} %get-tuple-element.231, s32[]{:T(128)S(6)} %select_n.54, bf16[4,128,2304]{2,1,0:T(8,128)(2,1)S(1)} %get-tuple-element.229), kind=kOutput, calls=%fused_computation.12.clone.1 | convolution fusion | flops 1208221696 | bytes 12125184 | tf_op jit(solution)/shard_map/while/body/dot_general | solution.py:34
  288.2 9.0 %fusion.22 = f32[128,64]{1,0:T(8,128)S(1)} fusion(f32[128,2048]{1,0:T(8,128)S(1)} %get-tuple-element.60, s32[2048]{0:T(1024)S(1)} %iota_add_fusion, s32[128,64]{1,0:T(8,128)S(1)} %copy.23), kind=kLoop, calls=%fused_computation.22 | loop fusion | flops 50323456 | bytes 1122304 | tf_op jit(solution)/shard_map/reduce_sum | solution.py:80
  297.2 0.1 copy.28
  297.4 0.0 copy-start.3
  297.4 0.6 copy-done.3
  298.0 0.0 all-gather.2.cloned.1.call-update
  298.0 0.0 copy-start.1
  298.1 57.9 %copy.29 = bf16[2048,4,2304]{2,1,0:T(4,128)(2,1)} copy(bf16[2048,4,2304]{0,2,1:T(8,128)(2,1)} %get-tuple-element.101) | data formatting | bytes 75497472
  355.9 0.5 broadcast_multiply_fusion
  356.4 0.8 all-gather.2.cloned.1.call-done
  357.2 3.1 reduce_sum.39
  (8 shorter events, 0.1 us)
Async XLA Ops:
  7.2 26.8 %copy-start = (s32[4,128,64]{1,2,0:T(8,128)S(1)}, s32[4,128,64]{1,2,0:T(8,128)}, u32[]{:S(2)}) copy-start(s32[4,128,64]{1,2,0:T(8,128)} %param.10) | copy-start | bytes 393220
  7.2 212.0 %all-reduce.2.cloned.1.call-start = ((), (), s32[]{:S(2)}) async-start(), calls=%async_computation | async-start | bytes 9437184 | tf_op jit(solution)/shard_map/psum | solution.py:62
  46.5 172.7 %copy-start.4 = (f32[4,2304]{1,0:T(4,128)S(1)}, f32[4,2304]{1,0:T(4,128)}, u32[]{:S(2)}) copy-start(f32[4,2304]{1,0:T(4,128)} %param.12) | copy-start | bytes 110596
  73.4 149.9 %copy-start.2 = (bf16[128,2048]{1,0:T(8,128)(2,1)}, bf16[128,2048]{1,0:T(8,128)(2,1)S(1)}, u32[]{:S(2)}) copy-start(bf16[128,2048]{1,0:T(8,128)(2,1)S(1)} %get-tuple-element.240) | copy-start | bytes 1572868
  73.4 283.8 %all-gather.2.cloned.1.call-start = ((), (), s32[]{:S(2)}) async-start(), calls=%async_computation.1 | async-start | bytes 4325376 | tf_op jit(solution)/shard_map/all_gather | solution.py:14
  297.4 0.7 copy-start.3
  298.0 62.2 %copy-start.1 = (s32[4,128,64]{1,2,0:T(8,128)S(1)}, s32[4,128,64]{1,2,0:T(8,128)}, u32[]{:S(2)}) copy-start(s32[4,128,64]{1,2,0:T(8,128)} %param.10) | copy-start | bytes 393220
Sparse Core Ops, SparseCore 0:
  73.5 145.6 all-reduce.1
  298.2 58.9 all-gather.1
